TPU v7x, 32 devices: a whole 2x2x4 slice. The times are simulated.
32 devices in a mesh: row: 4 (over x, core), col: 8 (over z, y).
Axes of the slice: x: 2, y: 2, z: 4, core: 2. Of those that a mesh axis runs over, the one named last changes fastest.
Arguments:
- normed: bfloat16 [12288, 6144], P(('row', 'col')), may hold values from -6 to 6
- out_grad: bfloat16 [12288, 6144], P(('row', 'col')), may hold values from -0.125 to 0.125
- w_in: bfloat16 [6144, 48], replicated, may hold values from -0.078125 to 0.078125
- hidden_grad: bfloat16 [12288, 48], P(('row', 'col')), may hold values from -0.125 to 0.125
- qkv_grad: bfloat16 [12288, 64], P(('row', 'col')), may hold values from -0.125 to 0.125
- bucket_order: int32 [160], replicated, may hold values from 0 to 159, each once
Outputs:
- buckets: bfloat16 [160, 6144], replicated
Inputs may be any that keep to these rules, and one draw needn't show every extreme that they name: bucket_order is a permutation of 0 to 159.
All inputs are finite; a program needn't handle non-finite values.
Results may differ from a plain program's by a relative error of at most 0.0044.
Values may be sent and summed in bfloat16 or wider, within the bound.
A program may use at most 64 MiB of HBM per device.

v0:
```python
import jax
import jax.numpy as jnp
from jax import lax
from jax.sharding import PartitionSpec as P

NB = 4


def local(normed, out_grad, w_in, hidden_grad, qkv_grad, bucket_order):
    pre = jnp.dot(normed, w_in, preferred_element_type=jnp.float32)
    cdf = 0.5 * (1.0 + lax.erf(pre * 0.7071067811865476))
    pdf = jnp.exp(-0.5 * pre * pre) * 0.3989422804014327
    hidden = (pre * cdf).astype(jnp.bfloat16)
    pre_grad = (hidden_grad.astype(jnp.float32) * (cdf + pre * pdf)).astype(jnp.bfloat16)
    grad_qkv = jnp.dot(qkv_grad.T, normed, preferred_element_type=jnp.float32)
    grad_in = jnp.dot(pre_grad.T, normed, preferred_element_type=jnp.float32)
    grad_out = jnp.dot(hidden.T, out_grad, preferred_element_type=jnp.float32)
    stacked = jnp.concatenate([grad_qkv, grad_in, grad_out], axis=0)
    ordered = jnp.take(stacked, bucket_order, axis=0)
    per_bucket = ordered.shape[0] // NB
    results = []
    for bucket in range(NB):
        piece = ordered[bucket * per_bucket : (bucket + 1) * per_bucket]
        summed = lax.psum(piece, ("row", "col")).astype(jnp.bfloat16)
        results.append(summed)
    return jnp.concatenate(results, axis=0)


def solution(mesh):
    in_specs = (
        P(("row", "col"), None),
        P(("row", "col"), None),
        P(),
        P(("row", "col"), None),
        P(("row", "col"), None),
        P(),
    )
    out_specs = P()
    return jax.shard_map(local, mesh=mesh, in_specs=in_specs, out_specs=out_specs, check_vma=False)
```

profile of v0, /device:TPU:0, one launch (start us, length us, event | category | flops | bytes accessed | tf_op | source)
XLA Modules:
  0.0 118.2 jit_solution(10145399101433720630)
XLA Ops:
  0.0 0.0 copy-start
  0.0 0.0 copy-start.2
  0.0 1.1 copy-done
  1.1 4.3 %fusion.15 = f32[384,48]{0,1:T(8,128)S(1)} fusion(bf16[384,6144]{1,0:T(8,128)(2,1)} %param.6, bf16[6144,48]{0,1:T(8,128)(2,1)S(1)} %copy-done), kind=kOutput, calls=%fused_computation.24 | convolution fusion | flops 226492416 | bytes 5382144 | tf_op jit(solution)/shard_map/dot_general | solution.py:10
  5.4 0.0 copy-done.2
  5.4 0.0 copy-start.1
  5.4 0.0 copy-start.4
  5.4 0.9 fusion.6
  6.4 1.4 %copy-done.1 = bf16[384,6144]{1,0:T(8,128)(2,1)S(1)} copy-done((bf16[384,6144]{1,0:T(8,128)(2,1)S(1)}, bf16[384,6144]{1,0:T(8,128)(2,1)}, u32[]{:S(2)}) %copy-start.1) | copy-done | bytes 4718616
  7.7 0.0 copy-done.4
  7.7 0.0 copy-start.3
  7.7 0.9 fusion.7
  8.7 0.0 copy-done.3
  8.7 0.9 fusion.14
  9.6 0.0 copy-start.5
  9.7 2.1 %pad_maximum_fusion = f32[160,6144]{1,0:T(8,128)} fusion(f32[48,6144]{1,0:T(8,128)S(1)} %fusion.6, f32[48,6144]{1,0:T(8,128)S(1)} %fusion.7, f32[64,6144]{1,0:T(8,128)S(1)} %fusion.14), kind=kLoop, calls=%fused_computation.1 | loop fusion | flops 1966080 | bytes 7864320 | tf_op jit(solution)/shard_map/concatenate | solution.py:18
  11.8 0.0 copy-done.5
  11.8 7.4 %gather_fusion = f32[160,6144]{1,0:T(8,128)} fusion(f32[160,6144]{1,0:T(8,128)} %pad_maximum_fusion, s32[1024]{0:T(1024)S(1)} %pad_clamp_fusion), kind=kCustom, calls=%fused_computation | custom fusion | bytes 7864960 | tf_op jit(solution)/shard_map/jit(_take)/gather | solution.py:19
  19.3 2.7 %broadcast_select_fusion = f32[160,6144]{1,0:T(8,128)S(1)} fusion(f32[160,6144]{1,0:T(8,128)} %gather_fusion, pred[160]{0:T(512)(128)(4,1)S(1)} %compare_and_fusion), kind=kLoop, calls=%fused_computation.3 | loop fusion | flops 983040 | bytes 7864480 | tf_op jit(solution)/shard_map/jit(_take)/select_n | solution.py:19
  22.0 1.2 %fusion.13 = (f32[40,6144]{1,0:T(8,128)S(1)}, f32[40,6144]{1,0:T(8,128)S(1)}, f32[40,6144]{1,0:T(8,128)S(1)}, f32[40,6144]{1,0:T(8,128)}) fusion(f32[160,6144]{1,0:T(8,128)S(1)} %broadcast_select_fusion), kind=kLoop, calls=%fused_computation.22 | loop fusion | bytes 7864320 | tf_op jit(solution)/shard_map/slice | solution.py:23
  23.2 92.1 %all-reduce.2 = (bf16[40,6144]{1,0:T(8,128)(2,1)}, bf16[40,6144]{1,0:T(8,128)(2,1)}, bf16[40,6144]{1,0:T(8,128)(2,1)}, bf16[40,6144]{1,0:T(8,128)(2,1)}) all-reduce(f32[40,6144]{1,0:T(8,128)S(1)} %get-tuple-element.10, f32[40,6144]{1,0:T(8,128)S(1)} %get-tuple-element.11, ...), channel_id=1, replica_groups=mesh['row'=4,'col'=8] {'row','col'}, use_global_device_ids=true, to_apply=%region_3.4 | all-reduce | flops 983040 | bytes 5898240 | tf_op jit(solution)/shard_map/psum | solution.py:24
  115.3 2.9 %pad_maximum_fusion.1 = bf16[160,6144]{1,0:T(8,128)(2,1)} fusion(bf16[40,6144]{1,0:T(8,128)(2,1)} %get-tuple-element.5, bf16[40,6144]{1,0:T(8,128)(2,1)} %get-tuple-element.6, bf16[40,6144]{1,0:T(8,128)(2,1)} %get-tuple-element.7, bf16[40,6144]{1,0:T(8,128)(2,1)} %get-tuple-element.8), kind=kLoop, calls=%fused_computation.2 | loop fusion | flops 7864320 | bytes 3932160 | tf_op jit(solution)/shard_map/concatenate | solution.py:26
  (3 shorter events, 0.0 us)
Async XLA Ops:
  0.0 1.1 copy-start
  0.0 5.4 %copy-start.2 = (bf16[384,6144]{1,0:T(8,128)(2,1)S(1)}, bf16[384,6144]{1,0:T(8,128)(2,1)}, u32[]{:S(2)}) copy-start(bf16[384,6144]{1,0:T(8,128)(2,1)} %param.7) | copy-start | bytes 14155780
  5.4 2.3 %copy-start.1 = (bf16[384,6144]{1,0:T(8,128)(2,1)S(1)}, bf16[384,6144]{1,0:T(8,128)(2,1)}, u32[]{:S(2)}) copy-start(bf16[384,6144]{1,0:T(8,128)(2,1)} %param.6) | copy-start | bytes 14155780
  5.4 2.3 %copy-start.4 = (bf16[384,48]{0,1:T(8,128)(2,1)S(1)}, bf16[384,48]{0,1:T(8,128)(2,1)}, u32[]{:S(2)}) copy-start(bf16[384,48]{0,1:T(8,128)(2,1)} %param.9) | copy-start | bytes 110596
  7.7 0.9 copy-start.3
  9.6 2.2 %copy-start.5 = (s32[160]{0:T(256)S(1)}, s32[160]{0:T(256)}, u32[]{:S(2)}) copy-start(s32[160]{0:T(256)} %param.11) | copy-start | bytes 1924
where the time goes:
time: 118 us
  blocking collectives  92.1 us (78%)
  local copies, waits for them, and re-layouts  11.1 us (9%)
  other arithmetic  7.78 us (7%)
  matrix products  7.13 us (6%)
    psum x1, blocking collectives, local(): summed = lax.psum(piece, ('row', 'col')).astype(jnp.bfloat16)  92.1 us
    gather x1, local copies, waits for them, and re-layouts, local(): ordered = jnp.take(stacked, bucket_order, axis=0)  7.44 us
    dot_general x1, matrix products, local(): pre = jnp.dot(normed, w_in, preferred_element_type=jnp.float32)  4.31 us
    concatenate x1, other arithmetic, local(): return jnp.concatenate(results, axis=0)  2.92 us
    select_n x2, other arithmetic, local(): ordered = jnp.take(stacked, bucket_order, axis=0)  2.7 us
    unnamed x12, local copies, waits for them, and re-layouts  2.46 us

commit v1 on v0

--- a/solution.py
+++ b/solution.py
@@ -21,7 +21,11 @@
     results = []
     for bucket in range(NB):
         piece = ordered[bucket * per_bucket : (bucket + 1) * per_bucket]
-        summed = lax.psum(piece, ("row", "col")).astype(jnp.bfloat16)
+
+        def _update_series(m):
+            return lax.psum(lax.psum(m, axis_name="col"), axis_name="row")
+
+        summed = _update_series(piece).astype(jnp.bfloat16)
         results.append(summed)
     return jnp.concatenate(results, axis=0)
 

time: 118 us -> 264 us (2.24)
  waiting for transfers between devices: 0 us -> 152 us
  blocking collectives: 92.1 us -> 72.4 us
  between operations: 0.08 us -> 13.5 us
    psum x0 -> x1, waiting for transfers between devices: none -> 152 us  [_update_series(): return lax.psum(lax.psum(m, axis_name='col'), axis_name='row')]
    psum x1, blocking collectives: 92.1 us -> 72.4 us  [_update_series(): return lax.psum(lax.psum(m, axis_name='col'), axis_name='row')]
  transfers between devices with their start and end apart: 0 -> 1, of which waited for: 0 -> 1; matrix products, arithmetic and copies ran while one was open for 0% -> 0% of each run, Pallas kernels for 0% -> 0%
where the time goes in v1:
time: 264 us
  waiting for transfers between devices  152 us (58%)
  blocking collectives  72.4 us (27%)
  between operations  13.5 us (5%)
  local copies, waits for them, and re-layouts  10.8 us (4%)
  other arithmetic  8.19 us (3%)
  matrix products  6.64 us (3%)
    psum x1, waiting for transfers between devices, _update_series(): return lax.psum(lax.psum(m, axis_name='col'), axis_name='row')  152 us
    psum x1, blocking collectives, _update_series(): return lax.psum(lax.psum(m, axis_name='col'), axis_name='row')  72.4 us
    gather x1, local copies, waits for them, and re-layouts, local(): ordered = jnp.take(stacked, bucket_order, axis=0)  7.44 us
  transfers between devices with their start and end apart: 1, of which 1 were waited for; matrix products, arithmetic and copies ran while one was open for 0% of the time, Pallas kernels for 0%

profile of v1, /device:TPU:0, one launch (start us, length us, event | category | flops | bytes accessed | tf_op | source)
XLA Modules:
  0.0 264.0 jit_solution(742018976522438746)
XLA Ops:
  6.5 0.0 copy-start
  6.5 0.0 all-reduce.5.cloned.1.call-start
  6.5 0.0 copy-start.2
  6.5 0.8 compare_select_fusion
  7.4 1.1 compare_and_fusion
  8.5 0.0 copy-done
  8.5 3.8 %fusion.15 = f32[384,48]{0,1:T(8,128)S(1)} fusion(bf16[384,6144]{1,0:T(8,128)(2,1)} %param.6, bf16[6144,48]{0,1:T(8,128)(2,1)S(1)} %copy-done), kind=kOutput, calls=%fused_computation.24 | convolution fusion | flops 226492416 | bytes 5382144 | tf_op jit(solution)/shard_map/dot_general | solution.py:10
  12.3 0.0 copy-done.2
  12.3 0.0 copy-start.1
  12.3 0.0 copy-start.4
  12.3 0.9 fusion.6
  13.3 1.4 copy-done.1
  14.6 0.0 copy-done.4
  14.6 0.9 fusion.7
  15.6 0.0 copy-done.3
  15.6 0.9 fusion.14
  16.6 2.2 pad_maximum_fusion
  18.7 7.4 %gather_fusion = f32[160,6144]{1,0:T(8,128)} fusion(f32[160,6144]{1,0:T(8,128)} %pad_maximum_fusion, s32[1024]{0:T(1024)S(1)} %pad_clamp_fusion), kind=kCustom, calls=%fused_computation | custom fusion | bytes 7864960 | tf_op jit(solution)/shard_map/jit(_take)/gather | solution.py:19
  26.2 2.7 %broadcast_select_fusion = f32[160,6144]{1,0:T(8,128)S(1)} fusion(f32[160,6144]{1,0:T(8,128)} %gather_fusion, pred[160]{0:T(512)(128)(4,1)S(1)} %compare_and_fusion), kind=kLoop, calls=%fused_computation.3 | loop fusion | flops 983040 | bytes 7864480 | tf_op jit(solution)/shard_map/jit(_take)/select_n | solution.py:19
  28.9 2.0 fusion.13
  30.9 0.0 all-reduce.5.cloned.1.call-update
  30.9 152.4 %all-reduce.5.cloned.1.call-done = (f32[40,6144]{1,0:T(8,128)}, f32[40,6144]{1,0:T(8,128)}, f32[40,6144]{1,0:T(8,128)}, f32[40,6144]{1,0:T(8,128)}) async-done(((f32[40,6144]{1,0:T(8,128)}, f32[40,6144]{1,0:T(8,128)}, f32[40,6144]{1,0:T(8,128)}, f32[40,6144]{1,0:T(8,128)}), (f32[40,6144]{1,0:T(8,128)}, f32[40,6144]{1,0:T(8,128)}, f32[40,6144]{1,0:T(8,128)}, ...) | async-done | bytes 3932176 | tf_op jit(solution)/shard_map/psum | solution.py:26
  183.3 72.4 %all-reduce.6 = (bf16[40,6144]{1,0:T(8,128)(2,1)S(1)}, bf16[40,6144]{1,0:T(8,128)(2,1)S(1)}, bf16[40,6144]{1,0:T(8,128)(2,1)S(1)}, bf16[40,6144]{1,0:T(8,128)(2,1)S(1)}) all-reduce(f32[40,6144]{1,0:T(8,128)} %get-tuple-element.5, f32[40,6144]{1,0:T(8,128)} %get-tuple-element.6, ...), channel_id=1, replica_groups=mesh['row'=4,'col'=8] {'row'}, use_global_device_ids=true, to_apply=%region_7.8 | all-reduce | flops 983040 | bytes 5898240 | tf_op jit(solution)/shard_map/psum | solution.py:26
  255.7 1.4 pad_maximum_fusion.1
  (2 shorter events, 0.0 us)
Async XLA Ops:
  6.5 1.9 copy-start
  6.5 176.8 %all-reduce.5.cloned.1.call-start = ((), (), s32[]{:S(2)}) async-start(), calls=%async_computation | async-start | bytes 7864320 | tf_op jit(solution)/shard_map/psum | solution.py:26
  6.5 5.8 %copy-start.2 = (bf16[384,6144]{1,0:T(8,128)(2,1)S(1)}, bf16[384,6144]{1,0:T(8,128)(2,1)}, u32[]{:S(2)}) copy-start(bf16[384,6144]{1,0:T(8,128)(2,1)} %param.7) | copy-start | bytes 14155780
  12.3 2.3 copy-start.1
  12.3 2.3 copy-start.4
  14.6 0.9 copy-start.3
Sparse Core Ops, SparseCore 0:
  31.0 152.2 all-reduce.4
